TPU v7x, 32 devices: a whole 2x2x4 slice. The times are simulated.
32 devices in a mesh: row: 4 (over y, x), col: 8 (over z, core).
Axes of the slice: x: 2, y: 2, z: 4, core: 2. Of those that a mesh axis runs over, the one named last changes fastest.
Arguments:
- voltages: bfloat16 [4096, 32, 2, 256], P(('col', 'row')), may hold values from -6 to 6
- auto_prev: float32 [32, 4096], P('row', 'col'), may hold values from 0.5 to 8
- station_order: int32 [4096], replicated, may hold values from 0 to 4095, each once
Outputs:
- visibilities: bfloat16 [32, 5, 4096, 1024], P('row', None, 'col')
Inputs may be any that keep to these rules, and one draw needn't show every extreme that they name: `station_order`: a permutation of the block positions.
All inputs are finite; a program needn't handle non-finite values.
Results may differ from a plain program's by a relative error of at most 0.001.
Values may be sent and summed in bfloat16 or wider, within the bound.
No kernel may reach another device: no remote copies, remote signals or barrier semaphores. Data moves between devices by JAX's collectives and lax.ppermute only.
A program may use at most 192 MiB of HBM per device.

v0:
```python
import jax
import jax.numpy as jnp
from jax import lax
from jax.sharding import PartitionSpec as P

SAMPLES = 256


def from_behind(value, axis, by):
    count = lax.axis_size(axis)
    return lax.ppermute(value, axis, [(i, (i + by) % count) for i in range(count)])


def per_device(voltages, auto_prev, station_order):
    local = lax.all_to_all(voltages, "row", split_axis=1, concat_axis=0, tiled=True)
    block_size, chan_count, _, sample_count = local.shape
    blocks_count = lax.axis_size("col")
    offsets = blocks_count // 2 + 1
    block_index = lax.axis_index("col")
    autos_all = lax.all_gather(auto_prev, "col", axis=1, tiled=True)
    inverse = 1.0 / jnp.sqrt(jnp.take(autos_all, station_order, axis=1))
    row_scale = lax.dynamic_slice_in_dim(inverse, block_index * block_size, block_size, 1)
    own_rows = jnp.transpose(local.reshape(block_size, chan_count, 2 * sample_count), (1, 0, 2))
    own_turned = jnp.concatenate(
        [own_rows[:, :, sample_count:], -own_rows[:, :, :sample_count]], axis=-1
    )
    tiles = []
    partner = own_rows
    for offset in range(offsets):
        if offset > 0:
            partner = from_behind(partner, "col", 1)
        real_part = jnp.einsum(
            "cih,cjh->cij", own_rows, partner, preferred_element_type=jnp.float32
        )
        imag_part = jnp.einsum(
            "cih,cjh->cij", own_turned, partner, preferred_element_type=jnp.float32
        )
        start = (block_index - offset) % blocks_count * block_size
        column_scale = lax.dynamic_slice_in_dim(inverse, start, block_size, 1)
        factor = row_scale[:, :, None] * column_scale[:, None, :] * (1.0 / SAMPLES)
        tiles.append(
            jnp.concatenate([real_part * factor, imag_part * factor], axis=-1).astype(jnp.bfloat16)
        )
    return jnp.stack(tiles, axis=1)


def solution(mesh):
    return jax.shard_map(
        per_device,
        mesh=mesh,
        in_specs=(P(("col", "row"), None, None, None), P("row", "col"), P()),
        out_specs=P("row", None, "col", None),
        check_vma=False,
    )
```

profile of v0, /device:TPU:0, one launch (start us, length us, event | category | flops | bytes accessed | tf_op | source)
XLA Modules:
  0.0 391.6 jit_solution(7520869197970000974)
XLA Ops:
  0.0 8.6 %copy.13 = bf16[128,32,2,256]{3,2,0,1:T(2,128)(2,1)} copy(bf16[128,32,2,256]{3,2,1,0:T(2,128)(2,1)} %param.3) | data formatting | bytes 8388608 | tf_op args[0]
  8.6 53.2 %all_to_all.15 = bf16[128,32,2,256]{3,2,0,1:T(2,128)(2,1)S(1)} all-to-all(bf16[128,32,2,256]{3,2,0,1:T(2,128)(2,1)} %copy.13), channel_id=1, replica_groups=mesh['row'=4,'col'=8] {'row'}, dimensions={1} | all-to-all | bytes 8388608 | tf_op jit(solution)/shard_map/all_to_all | solution.py:15
  61.7 5.5 %copy.24 = bf16[128,4,8,2,256]{4,3,0,1,2:T(2,128)(2,1)} copy(bf16[128,4,8,2,256]{4,3,0,2,1:T(2,128)(2,1)S(1)} %bitcast.61) | data formatting | bytes 8388608 | tf_op jit(solution)/shard_map/all_to_all | solution.py:15
  67.2 7.6 %reshape.170 = bf16[512,8,512]{2,0,1:T(8,128)(2,1)} reshape(bf16[4,128,8,2,256]{4,3,1,0,2:T(2,128)(2,1)} %bitcast.62) | data formatting | bytes 8388608 | tf_op jit(solution)/shard_map/reshape | solution.py:23
  74.8 50.0 %collective-permute-done = bf16[8,512,512]{2,1,0:T(8,128)(2,1)} collective-permute-done((bf16[8,512,512]{2,1,0:T(8,128)(2,1)}, bf16[8,512,512]{2,1,0:T(8,128)(2,1)}, u32[]{:S(2)}, u32[]{:S(2)}) %collective-permute-start) | collective-permute-done | bytes 4194336 | tf_op jit(solution)/shard_map/ppermute | solution.py:11
  125.0 66.9 %all_gather.3 = f32[8,4096]{0,1:T(8,128)S(1)} all-gather(f32[8,512]{0,1:T(8,128)S(1)} %copy.15), channel_id=1, replica_groups=mesh['row'=4,'col'=8] {'col'}, dimensions={1}, use_global_device_ids=true | all-gather | bytes 147456 | tf_op jit(solution)/shard_map/all_gather | solution.py:20
  191.9 14.2 %gather_fusion = f32[4096,8]{1,0:T(8,128)} fusion(f32[8,4096]{0,1:T(8,128)S(1)} %all_gather.3, s32[4096]{0:T(1024)S(1)} %fusion.10), kind=kCustom, calls=%fused_computation | custom fusion | bytes 278528 | tf_op jit(solution)/shard_map/jit(_take)/gather | solution.py:21
  210.5 7.9 %fusion = bf16[8,1,512,512]{2,3,0,1:T(8,128)(2,1)} fusion(f32[8,512]{1,0:T(8,128)S(1)} %copy.17, f32[8,512]{1,0:T(8,128)S(1)} %copy.16, bf16[512,8,512]{2,0,1:T(8,128)(2,1)} %reshape.170), kind=kOutput, calls=%fused_computation.21 | convolution fusion | flops 2155872256 | bytes 8421376 | tf_op jit(solution)/shard_map/cih,cjh->cij/dot_general | solution.py:32
  224.1 7.2 %maximum_dynamic-update-slice_fusion.4 = bf16[8,5,512,1024]{2,3,0,1:T(8,128)(2,1)} fusion(bf16[8,1,512,512]{2,3,0,1:T(8,128)(2,1)} %fusion.1, bf16[8,1,512,512]{2,3,0,1:T(8,128)(2,1)} %fusion), kind=kLoop, calls=%fused_computation.5 | loop fusion | flops 16777215 | bytes 16777216
  231.4 7.4 %fusion.3 = bf16[8,1,512,512]{2,3,0,1:T(8,128)(2,1)} fusion(f32[8,512]{1,0:T(8,128)S(1)} %copy.18, f32[8,512]{1,0:T(8,128)S(1)} %copy.16, bf16[8,512,512]{2,1,0:T(8,128)(2,1)} %collective-permute-done, bf16[8,512,256]{2,1,0:T(8,128)(2,1)} %copy-done.5, bf16[8,512,256]{2,1,0:T(8,128)(2,1)S(1)} %get-tuple-element.5), kind=kOutput, calls=%fused_computation.24 | convolution fusion | flops 2164260864 | bytes 12615680 | tf_op jit(solution)/shard_map/cih,cjh->cij/dot_general | solution.py:35
  238.7 6.5 %fusion.2 = bf16[8,1,512,512]{2,3,0,1:T(8,128)(2,1)} fusion(f32[8,512]{1,0:T(8,128)S(1)} %copy.18, f32[8,512]{1,0:T(8,128)S(1)} %copy.16, bf16[8,512,512]{2,1,0:T(8,128)(2,1)} %collective-permute-done, bf16[512,8,512]{2,0,1:T(8,128)(2,1)S(1)} %copy-done.1), kind=kOutput, calls=%fused_computation.23 | convolution fusion | flops 2155872256 | bytes 12615680 | tf_op jit(solution)/shard_map/cih,cjh->cij/dot_general | solution.py:32
  245.2 7.2 %maximum_dynamic-update-slice_fusion.3 = bf16[8,5,512,1024]{2,3,0,1:T(8,128)(2,1)} fusion(bf16[8,5,512,1024]{2,3,0,1:T(8,128)(2,1)} %maximum_dynamic-update-slice_fusion.4, bf16[8,1,512,512]{2,3,0,1:T(8,128)(2,1)} %fusion.3, bf16[8,1,512,512]{2,3,0,1:T(8,128)(2,1)} %fusion.2), kind=kLoop, calls=%fused_computation.4 | loop fusion | flops 16777216 | bytes 16777216
  252.5 16.0 %collective-permute-done.2 = bf16[8,512,512]{2,1,0:T(8,128)(2,1)} collective-permute-done((bf16[8,512,512]{2,1,0:T(8,128)(2,1)}, bf16[8,512,512]{2,1,0:T(8,128)(2,1)}, u32[]{:S(2)}, u32[]{:S(2)}) %collective-permute-start.2) | collective-permute-done | bytes 4194336 | tf_op jit(solution)/shard_map/ppermute | solution.py:11
  268.5 7.2 %fusion.5 = bf16[8,1,512,512]{2,3,0,1:T(8,128)(2,1)} fusion(f32[8,512]{1,0:T(8,128)S(1)} %copy.19, f32[8,512]{1,0:T(8,128)S(1)} %copy.16, bf16[8,512,512]{2,1,0:T(8,128)(2,1)} %collective-permute-done.1, bf16[8,512,256]{2,1,0:T(8,128)(2,1)} %copy-done.5, bf16[8,512,256]{2,1,0:T(8,128)(2,1)S(1)} %get-tuple-element.5), kind=kOutput, calls=%fused_computation.26 | convolution fusion | flops 2164260864 | bytes 12615680 | tf_op jit(solution)/shard_map/cih,cjh->cij/dot_general | solution.py:35
  275.7 6.5 %fusion.4 = bf16[8,1,512,512]{2,3,0,1:T(8,128)(2,1)} fusion(f32[8,512]{1,0:T(8,128)S(1)} %copy.19, f32[8,512]{1,0:T(8,128)S(1)} %copy.16, bf16[8,512,512]{2,1,0:T(8,128)(2,1)} %collective-permute-done.1, bf16[512,8,512]{2,0,1:T(8,128)(2,1)S(1)} %copy-done.2), kind=kOutput, calls=%fused_computation.25 | convolution fusion | flops 2155872256 | bytes 12615680 | tf_op jit(solution)/shard_map/cih,cjh->cij/dot_general | solution.py:32
  282.2 7.2 %maximum_dynamic-update-slice_fusion.2 = bf16[8,5,512,1024]{2,3,0,1:T(8,128)(2,1)} fusion(bf16[8,5,512,1024]{2,3,0,1:T(8,128)(2,1)} %maximum_dynamic-update-slice_fusion.3, bf16[8,1,512,512]{2,3,0,1:T(8,128)(2,1)} %fusion.5, bf16[8,1,512,512]{2,3,0,1:T(8,128)(2,1)} %fusion.4), kind=kLoop, calls=%fused_computation.3 | loop fusion | flops 16777216 | bytes 16777216
  289.4 7.4 %fusion.7 = bf16[8,1,512,512]{2,3,0,1:T(8,128)(2,1)} fusion(f32[8,512]{1,0:T(8,128)S(1)} %copy.20, f32[8,512]{1,0:T(8,128)S(1)} %copy.16, bf16[8,512,512]{2,1,0:T(8,128)(2,1)} %collective-permute-done.2, bf16[8,512,256]{2,1,0:T(8,128)(2,1)} %copy-done.5, bf16[8,512,256]{2,1,0:T(8,128)(2,1)S(1)} %get-tuple-element.5), kind=kOutput, calls=%fused_computation.28 | convolution fusion | flops 2164260864 | bytes 12615680 | tf_op jit(solution)/shard_map/cih,cjh->cij/dot_general | solution.py:35
  296.8 6.5 %fusion.6 = bf16[8,1,512,512]{2,3,0,1:T(8,128)(2,1)} fusion(f32[8,512]{1,0:T(8,128)S(1)} %copy.20, f32[8,512]{1,0:T(8,128)S(1)} %copy.16, bf16[8,512,512]{2,1,0:T(8,128)(2,1)} %collective-permute-done.2, bf16[512,8,512]{2,0,1:T(8,128)(2,1)S(1)} %copy-done.3), kind=kOutput, calls=%fused_computation.27 | convolution fusion | flops 2155872256 | bytes 12615680 | tf_op jit(solution)/shard_map/cih,cjh->cij/dot_general | solution.py:32
  303.3 7.2 %maximum_dynamic-update-slice_fusion.1 = bf16[8,5,512,1024]{2,3,0,1:T(8,128)(2,1)} fusion(bf16[8,5,512,1024]{2,3,0,1:T(8,128)(2,1)} %maximum_dynamic-update-slice_fusion.2, bf16[8,1,512,512]{2,3,0,1:T(8,128)(2,1)} %fusion.7, bf16[8,1,512,512]{2,3,0,1:T(8,128)(2,1)} %fusion.6), kind=kLoop, calls=%fused_computation.2 | loop fusion | flops 16777216 | bytes 16777216
  310.6 7.9 %collective-permute-done.3 = bf16[8,512,512]{2,1,0:T(8,128)(2,1)} collective-permute-done((bf16[8,512,512]{2,1,0:T(8,128)(2,1)}, bf16[8,512,512]{2,1,0:T(8,128)(2,1)}, u32[]{:S(2)}, u32[]{:S(2)}) %collective-permute-start.3) | collective-permute-done | bytes 4194336 | tf_op jit(solution)/shard_map/ppermute | solution.py:11
  318.5 7.2 %fusion.9 = bf16[8,1,512,512]{2,3,0,1:T(8,128)(2,1)} fusion(f32[8,512]{1,0:T(8,128)S(1)} %copy.21, f32[8,512]{1,0:T(8,128)S(1)} %copy.16, bf16[8,512,512]{2,1,0:T(8,128)(2,1)} %collective-permute-done.3, bf16[8,512,256]{2,1,0:T(8,128)(2,1)} %copy-done.5, bf16[8,512,256]{2,1,0:T(8,128)(2,1)S(1)} %get-tuple-element.5), kind=kOutput, calls=%fused_computation.30 | convolution fusion | flops 2164260864 | bytes 12615680 | tf_op jit(solution)/shard_map/cih,cjh->cij/dot_general | solution.py:35
  325.7 6.5 %fusion.8 = bf16[8,1,512,512]{2,3,0,1:T(8,128)(2,1)} fusion(f32[8,512]{1,0:T(8,128)S(1)} %copy.21, f32[8,512]{1,0:T(8,128)S(1)} %copy.16, bf16[8,512,512]{2,1,0:T(8,128)(2,1)} %collective-permute-done.3, bf16[512,8,512]{2,0,1:T(8,128)(2,1)S(1)} %copy-done.4), kind=kOutput, calls=%fused_computation.29 | convolution fusion | flops 2155872256 | bytes 12615680 | tf_op jit(solution)/shard_map/cih,cjh->cij/dot_general | solution.py:32
  332.2 7.2 %maximum_dynamic-update-slice_fusion = bf16[8,5,512,1024]{2,3,0,1:T(8,128)(2,1)} fusion(bf16[8,5,512,1024]{2,3,0,1:T(8,128)(2,1)} %maximum_dynamic-update-slice_fusion.1, bf16[8,1,512,512]{2,3,0,1:T(8,128)(2,1)} %fusion.9, bf16[8,1,512,512]{2,3,0,1:T(8,128)(2,1)} %fusion.8), kind=kLoop, calls=%fused_computation.1 | loop fusion | flops 16777216 | bytes 16777216 | tf_op jit(solution)/shard_map/stack | solution.py:44
  339.5 52.2 %copy.22 = bf16[8,5,512,1024]{3,2,1,0:T(8,128)(2,1)} copy(bf16[8,5,512,1024]{2,3,0,1:T(8,128)(2,1)} %maximum_dynamic-update-slice_fusion) | data formatting | bytes 83886080 | tf_op jit(solution)/shard_map/stack | solution.py:44
  (34 shorter events, 10.2 us)
Async XLA Ops:
  67.2 57.7 %copy-start.7 = (f32[8,512]{1,0:T(8,128)S(1)}, f32[8,512]{1,0:T(8,128)}, u32[]{:S(2)}) copy-start(f32[8,512]{1,0:T(8,128)} %param.4) | copy-start | bytes 49156
  67.2 124.7 %copy-start.6 = (s32[4096]{0:T(1024)S(1)}, s32[4096]{0:T(1024)}, u32[]{:S(2)}) copy-start(s32[4096]{0:T(1024)} %param.5) | copy-start | bytes 49156
  74.8 50.0 %collective-permute-start = (bf16[8,512,512]{2,1,0:T(8,128)(2,1)}, bf16[8,512,512]{2,1,0:T(8,128)(2,1)}, u32[]{:S(2)}, u32[]{:S(2)}) collective-permute-start(bf16[8,512,512]{2,1,0:T(8,128)(2,1)} %bitcast.59), channel_id=1, source_target_pairs={{0,1},{1,2},{2,3},{3,4},{4,5},{5,6},{6,7},{7,0},{8,9},{9,10},{10,1... | collective-permute-start | bytes 12582920 | tf_op jit(solution)/shard_map/ppermute | solution.py:11
  124.8 93.6 %collective-permute-start.1 = (bf16[8,512,512]{2,1,0:T(8,128)(2,1)}, bf16[8,512,512]{2,1,0:T(8,128)(2,1)}, u32[]{:S(2)}, u32[]{:S(2)}) collective-permute-start(bf16[8,512,512]{2,1,0:T(8,128)(2,1)} %collective-permute-done), channel_id=1, source_target_pairs={{0,1},{1,2},{2,3},{3,4},{4,5},{5,6},{6,7},{7,0},{8,9},{9,10},{10,1... | collective-permute-start | bytes 12582920 | tf_op jit(solution)/shard_map/ppermute | solution.py:11
  210.5 8.1 %copy-start = (bf16[512,8,512]{2,0,1:T(8,128)(2,1)S(1)}, bf16[512,8,512]{2,0,1:T(8,128)(2,1)}, u32[]{:S(2)}) copy-start(bf16[512,8,512]{2,0,1:T(8,128)(2,1)} %reshape.170) | copy-start | bytes 12582916
  218.4 50.0 %collective-permute-start.2 = (bf16[8,512,512]{2,1,0:T(8,128)(2,1)}, bf16[8,512,512]{2,1,0:T(8,128)(2,1)}, u32[]{:S(2)}, u32[]{:S(2)}) collective-permute-start(bf16[8,512,512]{2,1,0:T(8,128)(2,1)} %collective-permute-done.1), channel_id=1, source_target_pairs={{0,1},{1,2},{2,3},{3,4},{4,5},{5,6},{6,7},{7,0},{8,9},{9,10},{10,1... | collective-permute-start | bytes 12582920 | tf_op jit(solution)/shard_map/ppermute | solution.py:11
  218.9 1.4 copy-start.5
  231.4 7.4 %copy-start.1 = (bf16[512,8,512]{2,0,1:T(8,128)(2,1)S(1)}, bf16[512,8,512]{2,0,1:T(8,128)(2,1)}, u32[]{:S(2)}) copy-start(bf16[512,8,512]{2,0,1:T(8,128)(2,1)} %reshape.170) | copy-start | bytes 12582916
  252.5 23.2 %copy-start.2 = (bf16[512,8,512]{2,0,1:T(8,128)(2,1)S(1)}, bf16[512,8,512]{2,0,1:T(8,128)(2,1)}, u32[]{:S(2)}) copy-start(bf16[512,8,512]{2,0,1:T(8,128)(2,1)} %reshape.170) | copy-start | bytes 12582916
  268.5 50.0 %collective-permute-start.3 = (bf16[8,512,512]{2,1,0:T(8,128)(2,1)}, bf16[8,512,512]{2,1,0:T(8,128)(2,1)}, u32[]{:S(2)}, u32[]{:S(2)}) collective-permute-start(bf16[8,512,512]{2,1,0:T(8,128)(2,1)} %collective-permute-done.2), channel_id=1, source_target_pairs={{0,1},{1,2},{2,3},{3,4},{4,5},{5,6},{6,7},{7,0},{8,9},{9,10},{10,1... | collective-permute-start | bytes 12582920 | tf_op jit(solution)/shard_map/ppermute | solution.py:11
  289.4 7.4 %copy-start.3 = (bf16[512,8,512]{2,0,1:T(8,128)(2,1)S(1)}, bf16[512,8,512]{2,0,1:T(8,128)(2,1)}, u32[]{:S(2)}) copy-start(bf16[512,8,512]{2,0,1:T(8,128)(2,1)} %reshape.170) | copy-start | bytes 12582916
  310.6 15.2 %copy-start.4 = (bf16[512,8,512]{2,0,1:T(8,128)(2,1)S(1)}, bf16[512,8,512]{2,0,1:T(8,128)(2,1)}, u32[]{:S(2)}) copy-start(bf16[512,8,512]{2,0,1:T(8,128)(2,1)} %reshape.170) | copy-start | bytes 12582916
where the time goes:
time: 394 us; the launch traced here: 392 us
  blocking collectives  120 us (30%)
  local copies, waits for them, and re-layouts  90.2 us (23%)
  waiting for transfers between devices  74 us (19%)
  matrix products  67.1 us (17%)
  other arithmetic  40.1 us (10%)
    ppermute x4, waiting for transfers between devices, from_behind(): lax.ppermute(value, axis, [(i, (i + by) % count) for i in range(count)])  74 us
    all_gather x1, blocking collectives, per_device(): autos_all = lax.all_gather(auto_prev, 'col', axis=1, tiled=True)  66.9 us
    all_to_all x1, blocking collectives, per_device(): lax.all_to_all(voltages, 'row', split_axis=1, concat_axis=0, tiled=True)  53.2 us
    another operation x1, local copies, waits for them, and re-layouts, per_device(): return jnp.stack(tiles, axis=1)  52.2 us
    dot_general x5, matrix products, per_device(): jnp.einsum('cih,cjh->cij', own_rows, partner, preferred_element_type=jnp....  34 us
    dot_general x5, matrix products, per_device(): jnp.einsum('cih,cjh->cij', own_turned, partner, preferred_element_type=jn...  33.1 us
    unnamed x4, other arithmetic  28.9 us
    gather x1, local copies, waits for them, and re-layouts, per_device(): inverse = 1.0 / jnp.sqrt(jnp.take(autos_all, station_order, axis=1))  14.2 us
  transfers between devices with their start and end apart: 4, of which 3 were waited for; matrix products, arithmetic and copies ran while one was open for 26% of the time, Pallas kernels for 0%

commit v1 on v0

--- a/solution.py
+++ b/solution.py
@@ -17,7 +17,12 @@
     blocks_count = lax.axis_size("col")
     offsets = blocks_count // 2 + 1
     block_index = lax.axis_index("col")
-    autos_all = lax.all_gather(auto_prev, "col", axis=1, tiled=True)
+    ring = [auto_prev]
+    for hop in range(7):
+        ring.append(lax.ppermute(ring[-1], "col", [(dev, (dev + 1) % 8) for dev in range(8)]))
+    autos_all = jnp.roll(
+        jnp.concatenate(ring[::-1], axis=1), (lax.axis_index("col") + 1) * ring[0].shape[1], axis=1
+    )
     inverse = 1.0 / jnp.sqrt(jnp.take(autos_all, station_order, axis=1))
     row_scale = lax.dynamic_slice_in_dim(inverse, block_index * block_size, block_size, 1)
     own_rows = jnp.transpose(local.reshape(block_size, chan_count, 2 * sample_count), (1, 0, 2))

time: 394 us -> 375 us (0.952)
  blocking collectives: 120 us -> 53.2 us
  waiting for transfers between devices: 74 us -> 120 us
    ppermute x0 -> x7, waiting for transfers between devices: none -> 77.8 us  [per_device(): lax.ppermute(ring[-1], 'col', [(dev, (dev + 1) % 8) for dev in range(8)])]
    all_gather x1 -> x0, blocking collectives: 66.9 us -> none  [per_device(): autos_all = lax.all_gather(auto_prev, 'col', axis=1, tiled=True)]
    ppermute x4, waiting for transfers between devices: 74 us -> 41.9 us  [from_behind(): lax.ppermute(value, axis, [(i, (i + by) % count) for i in range(count)])]
    unnamed x18 -> x33, local copies, waits for them, and re-layouts: 10.1 us -> 10.6 us
  transfers between devices with their start and end apart: 4 -> 11, of which waited for: 3 -> 10; matrix products, arithmetic and copies ran while one was open for 26% -> 27% of each run, Pallas kernels for 0% -> 0%
where the time goes in v1:
time: 375 us; the launch traced here: 373 us
  waiting for transfers between devices  120 us (32%)
  local copies, waits for them, and re-layouts  90.8 us (24%)
  matrix products  67 us (18%)
  blocking collectives  53.2 us (14%)
  other arithmetic  40.1 us (11%)
    ppermute x7, waiting for transfers between devices, per_device(): lax.ppermute(ring[-1], 'col', [(dev, (dev + 1) % 8) for dev in range(8)])  77.8 us
    all_to_all x1, blocking collectives, per_device(): lax.all_to_all(voltages, 'row', split_axis=1, concat_axis=0, tiled=True)  53.2 us
    another operation x1, local copies, waits for them, and re-layouts, per_device(): return jnp.stack(tiles, axis=1)  52.2 us
    ppermute x4, waiting for transfers between devices, from_behind(): lax.ppermute(value, axis, [(i, (i + by) % count) for i in range(count)])  41.9 us
    dot_general x5, matrix products, per_device(): jnp.einsum('cih,cjh->cij', own_rows, partner, preferred_element_type=jnp....  34 us
    dot_general x5, matrix products, per_device(): jnp.einsum('cih,cjh->cij', own_turned, partner, preferred_element_type=jn...  33.1 us
    unnamed x4, other arithmetic  28.9 us
    gather x1, local copies, waits for them, and re-layouts, per_device(): inverse = 1.0 / jnp.sqrt(jnp.take(autos_all, station_order, axis=1))  14.2 us
  transfers between devices with their start and end apart: 11, of which 10 were waited for; matrix products, arithmetic and copies ran while one was open for 27% of the time, Pallas kernels for 0%

profile of v1, /device:TPU:0, one launch (start us, length us, event | category | flops | bytes accessed | tf_op | source)
XLA Modules:
  0.0 373.0 jit_solution(926021689959267682)
XLA Ops:
  0.0 8.6 %copy.15 = bf16[128,32,2,256]{3,2,0,1:T(2,128)(2,1)} copy(bf16[128,32,2,256]{3,2,1,0:T(2,128)(2,1)} %param.3) | data formatting | bytes 8388608 | tf_op args[0]
  8.6 53.2 %all_to_all.15 = bf16[128,32,2,256]{3,2,0,1:T(2,128)(2,1)S(1)} all-to-all(bf16[128,32,2,256]{3,2,0,1:T(2,128)(2,1)} %copy.15), channel_id=1, replica_groups=mesh['row'=4,'col'=8] {'row'}, dimensions={1} | all-to-all | bytes 8388608 | tf_op jit(solution)/shard_map/all_to_all | solution.py:15
  61.7 5.5 %copy.27 = bf16[128,4,8,2,256]{4,3,0,1,2:T(2,128)(2,1)} copy(bf16[128,4,8,2,256]{4,3,0,2,1:T(2,128)(2,1)S(1)} %bitcast.61) | data formatting | bytes 8388608 | tf_op jit(solution)/shard_map/all_to_all | solution.py:15
  67.2 7.6 %reshape.170 = bf16[512,8,512]{2,0,1:T(8,128)(2,1)} reshape(bf16[4,128,8,2,256]{4,3,1,0,2:T(2,128)(2,1)} %bitcast.62) | data formatting | bytes 8388608 | tf_op jit(solution)/shard_map/reshape | solution.py:28
  76.7 48.2 %collective-permute-done = f32[8,512]{1,0:T(8,128)S(1)} collective-permute-done((f32[8,512]{1,0:T(8,128)S(1)}, f32[8,512]{1,0:T(8,128)S(1)}, u32[]{:S(2)}, u32[]{:S(2)}) %collective-permute-start) | collective-permute-done | bytes 16416 | tf_op jit(solution)/shard_map/ppermute | solution.py:22
  155.5 14.2 %gather_fusion = f32[4096,8]{1,0:T(8,128)} fusion(f32[8,4096]{0,1:T(8,128)S(1)} %copy.25, s32[4096]{0:T(1024)S(1)} %fusion.10), kind=kCustom, calls=%fused_computation | custom fusion | bytes 278528 | tf_op jit(solution)/shard_map/jit(_take)/gather | solution.py:26
  174.1 7.9 %fusion = bf16[8,1,512,512]{2,3,0,1:T(8,128)(2,1)} fusion(f32[8,512]{1,0:T(8,128)S(1)} %copy.19, f32[8,512]{1,0:T(8,128)S(1)} %copy.18, bf16[512,8,512]{2,0,1:T(8,128)(2,1)} %reshape.170), kind=kOutput, calls=%fused_computation.21 | convolution fusion | flops 2155872256 | bytes 8421376 | tf_op jit(solution)/shard_map/cih,cjh->cij/dot_general | solution.py:37
  182.0 17.8 %collective-permute-done.8 = bf16[8,512,512]{2,1,0:T(8,128)(2,1)} collective-permute-done((bf16[8,512,512]{2,1,0:T(8,128)(2,1)}, bf16[8,512,512]{2,1,0:T(8,128)(2,1)}, u32[]{:S(2)}, u32[]{:S(2)}) %collective-permute-start.8) | collective-permute-done | bytes 4194336 | tf_op jit(solution)/shard_map/ppermute | solution.py:11
  205.3 7.2 %maximum_dynamic-update-slice_fusion.4 = bf16[8,5,512,1024]{2,3,0,1:T(8,128)(2,1)} fusion(bf16[8,1,512,512]{2,3,0,1:T(8,128)(2,1)} %fusion.1, bf16[8,1,512,512]{2,3,0,1:T(8,128)(2,1)} %fusion), kind=kLoop, calls=%fused_computation.5 | loop fusion | flops 16777215 | bytes 16777216
  212.6 7.4 %fusion.3 = bf16[8,1,512,512]{2,3,0,1:T(8,128)(2,1)} fusion(f32[8,512]{1,0:T(8,128)S(1)} %copy.20, f32[8,512]{1,0:T(8,128)S(1)} %copy.18, bf16[8,512,512]{2,1,0:T(8,128)(2,1)} %collective-permute-done.7, bf16[8,512,256]{2,1,0:T(8,128)(2,1)} %copy-done.5, bf16[8,512,256]{2,1,0:T(8,128)(2,1)S(1)} %get-tuple-element.5), kind=kOutput, calls=%fused_computation.24 | convolution fusion | flops 2164260864 | bytes 12615680 | tf_op jit(solution)/shard_map/cih,cjh->cij/dot_general | solution.py:40
  219.9 6.5 %fusion.2 = bf16[8,1,512,512]{2,3,0,1:T(8,128)(2,1)} fusion(f32[8,512]{1,0:T(8,128)S(1)} %copy.20, f32[8,512]{1,0:T(8,128)S(1)} %copy.18, bf16[8,512,512]{2,1,0:T(8,128)(2,1)} %collective-permute-done.7, bf16[512,8,512]{2,0,1:T(8,128)(2,1)S(1)} %copy-done.1), kind=kOutput, calls=%fused_computation.23 | convolution fusion | flops 2155872256 | bytes 12615680 | tf_op jit(solution)/shard_map/cih,cjh->cij/dot_general | solution.py:37
  226.4 7.2 %maximum_dynamic-update-slice_fusion.3 = bf16[8,5,512,1024]{2,3,0,1:T(8,128)(2,1)} fusion(bf16[8,5,512,1024]{2,3,0,1:T(8,128)(2,1)} %maximum_dynamic-update-slice_fusion.4, bf16[8,1,512,512]{2,3,0,1:T(8,128)(2,1)} %fusion.3, bf16[8,1,512,512]{2,3,0,1:T(8,128)(2,1)} %fusion.2), kind=kLoop, calls=%fused_computation.4 | loop fusion | flops 16777216 | bytes 16777216
  233.7 16.2 %collective-permute-done.9 = bf16[8,512,512]{2,1,0:T(8,128)(2,1)} collective-permute-done((bf16[8,512,512]{2,1,0:T(8,128)(2,1)}, bf16[8,512,512]{2,1,0:T(8,128)(2,1)}, u32[]{:S(2)}, u32[]{:S(2)}) %collective-permute-start.9) | collective-permute-done | bytes 4194336 | tf_op jit(solution)/shard_map/ppermute | solution.py:11
  249.8 7.2 %fusion.5 = bf16[8,1,512,512]{2,3,0,1:T(8,128)(2,1)} fusion(f32[8,512]{1,0:T(8,128)S(1)} %copy.21, f32[8,512]{1,0:T(8,128)S(1)} %copy.18, bf16[8,512,512]{2,1,0:T(8,128)(2,1)} %collective-permute-done.8, bf16[8,512,256]{2,1,0:T(8,128)(2,1)} %copy-done.5, bf16[8,512,256]{2,1,0:T(8,128)(2,1)S(1)} %get-tuple-element.5), kind=kOutput, calls=%fused_computation.26 | convolution fusion | flops 2164260864 | bytes 12615680 | tf_op jit(solution)/shard_map/cih,cjh->cij/dot_general | solution.py:40
  257.1 6.5 %fusion.4 = bf16[8,1,512,512]{2,3,0,1:T(8,128)(2,1)} fusion(f32[8,512]{1,0:T(8,128)S(1)} %copy.21, f32[8,512]{1,0:T(8,128)S(1)} %copy.18, bf16[8,512,512]{2,1,0:T(8,128)(2,1)} %collective-permute-done.8, bf16[512,8,512]{2,0,1:T(8,128)(2,1)S(1)} %copy-done.2), kind=kOutput, calls=%fused_computation.25 | convolution fusion | flops 2155872256 | bytes 12615680 | tf_op jit(solution)/shard_map/cih,cjh->cij/dot_general | solution.py:37
  263.6 7.2 %maximum_dynamic-update-slice_fusion.2 = bf16[8,5,512,1024]{2,3,0,1:T(8,128)(2,1)} fusion(bf16[8,5,512,1024]{2,3,0,1:T(8,128)(2,1)} %maximum_dynamic-update-slice_fusion.3, bf16[8,1,512,512]{2,3,0,1:T(8,128)(2,1)} %fusion.5, bf16[8,1,512,512]{2,3,0,1:T(8,128)(2,1)} %fusion.4), kind=kLoop, calls=%fused_computation.3 | loop fusion | flops 16777216 | bytes 16777216
  270.8 7.4 %fusion.7 = bf16[8,1,512,512]{2,3,0,1:T(8,128)(2,1)} fusion(f32[8,512]{1,0:T(8,128)S(1)} %copy.22, f32[8,512]{1,0:T(8,128)S(1)} %copy.18, bf16[8,512,512]{2,1,0:T(8,128)(2,1)} %collective-permute-done.9, bf16[8,512,256]{2,1,0:T(8,128)(2,1)} %copy-done.5, bf16[8,512,256]{2,1,0:T(8,128)(2,1)S(1)} %get-tuple-element.5), kind=kOutput, calls=%fused_computation.28 | convolution fusion | flops 2164260864 | bytes 12615680 | tf_op jit(solution)/shard_map/cih,cjh->cij/dot_general | solution.py:40
  278.2 6.5 %fusion.6 = bf16[8,1,512,512]{2,3,0,1:T(8,128)(2,1)} fusion(f32[8,512]{1,0:T(8,128)S(1)} %copy.22, f32[8,512]{1,0:T(8,128)S(1)} %copy.18, bf16[8,512,512]{2,1,0:T(8,128)(2,1)} %collective-permute-done.9, bf16[512,8,512]{2,0,1:T(8,128)(2,1)S(1)} %copy-done.3), kind=kOutput, calls=%fused_computation.27 | convolution fusion | flops 2155872256 | bytes 12615680 | tf_op jit(solution)/shard_map/cih,cjh->cij/dot_general | solution.py:37
  284.7 7.2 %maximum_dynamic-update-slice_fusion.1 = bf16[8,5,512,1024]{2,3,0,1:T(8,128)(2,1)} fusion(bf16[8,5,512,1024]{2,3,0,1:T(8,128)(2,1)} %maximum_dynamic-update-slice_fusion.2, bf16[8,1,512,512]{2,3,0,1:T(8,128)(2,1)} %fusion.7, bf16[8,1,512,512]{2,3,0,1:T(8,128)(2,1)} %fusion.6), kind=kLoop, calls=%fused_computation.2 | loop fusion | flops 16777216 | bytes 16777216
  292.0 7.9 %collective-permute-done.10 = bf16[8,512,512]{2,1,0:T(8,128)(2,1)} collective-permute-done((bf16[8,512,512]{2,1,0:T(8,128)(2,1)}, bf16[8,512,512]{2,1,0:T(8,128)(2,1)}, u32[]{:S(2)}, u32[]{:S(2)}) %collective-permute-start.10) | collective-permute-done | bytes 4194336 | tf_op jit(solution)/shard_map/ppermute | solution.py:11
  299.9 7.2 %fusion.9 = bf16[8,1,512,512]{2,3,0,1:T(8,128)(2,1)} fusion(f32[8,512]{1,0:T(8,128)S(1)} %copy.23, f32[8,512]{1,0:T(8,128)S(1)} %copy.18, bf16[8,512,512]{2,1,0:T(8,128)(2,1)} %collective-permute-done.10, bf16[8,512,256]{2,1,0:T(8,128)(2,1)} %copy-done.5, bf16[8,512,256]{2,1,0:T(8,128)(2,1)S(1)} %get-tuple-element.5), kind=kOutput, calls=%fused_computation.30 | convolution fusion | flops 2164260864 | bytes 12615680 | tf_op jit(solution)/shard_map/cih,cjh->cij/dot_general | solution.py:40
  307.1 6.5 %fusion.8 = bf16[8,1,512,512]{2,3,0,1:T(8,128)(2,1)} fusion(f32[8,512]{1,0:T(8,128)S(1)} %copy.23, f32[8,512]{1,0:T(8,128)S(1)} %copy.18, bf16[8,512,512]{2,1,0:T(8,128)(2,1)} %collective-permute-done.10, bf16[512,8,512]{2,0,1:T(8,128)(2,1)S(1)} %copy-done.4), kind=kOutput, calls=%fused_computation.29 | convolution fusion | flops 2155872256 | bytes 12615680 | tf_op jit(solution)/shard_map/cih,cjh->cij/dot_general | solution.py:37
  313.6 7.2 %maximum_dynamic-update-slice_fusion = bf16[8,5,512,1024]{2,3,0,1:T(8,128)(2,1)} fusion(bf16[8,5,512,1024]{2,3,0,1:T(8,128)(2,1)} %maximum_dynamic-update-slice_fusion.1, bf16[8,1,512,512]{2,3,0,1:T(8,128)(2,1)} %fusion.9, bf16[8,1,512,512]{2,3,0,1:T(8,128)(2,1)} %fusion.8), kind=kLoop, calls=%fused_computation.1 | loop fusion | flops 16777216 | bytes 16777216 | tf_op jit(solution)/shard_map/stack | solution.py:49
  320.8 52.2 %copy.24 = bf16[8,5,512,1024]{3,2,1,0:T(8,128)(2,1)} copy(bf16[8,5,512,1024]{2,3,0,1:T(8,128)(2,1)} %maximum_dynamic-update-slice_fusion) | data formatting | bytes 83886080 | tf_op jit(solution)/shard_map/stack | solution.py:49
  (64 shorter events, 42.1 us)
Async XLA Ops:
  67.2 7.6 %copy-start.7 = (f32[8,512]{1,0:T(8,128)S(1)}, f32[8,512]{1,0:T(8,128)}, u32[]{:S(2)}) copy-start(f32[8,512]{1,0:T(8,128)} %param.4) | copy-start | bytes 49156
  67.2 77.6 %copy-start.6 = (s32[4096]{0:T(1024)S(1)}, s32[4096]{0:T(1024)}, u32[]{:S(2)}) copy-start(s32[4096]{0:T(1024)} %param.5) | copy-start | bytes 49156
  74.8 74.9 %collective-permute-start.7 = (bf16[8,512,512]{2,1,0:T(8,128)(2,1)}, bf16[8,512,512]{2,1,0:T(8,128)(2,1)}, u32[]{:S(2)}, u32[]{:S(2)}) collective-permute-start(bf16[8,512,512]{2,1,0:T(8,128)(2,1)} %bitcast.59), channel_id=1, source_target_pairs={{0,1},{1,2},{2,3},{3,4},{4,5},{5,6},{6,7},{7,0},{8,9},{9,10},{10,1... | collective-permute-start | bytes 12582920 | tf_op jit(solution)/shard_map/ppermute | solution.py:11
  74.8 50.1 %collective-permute-start = (f32[8,512]{1,0:T(8,128)S(1)}, f32[8,512]{1,0:T(8,128)S(1)}, u32[]{:S(2)}, u32[]{:S(2)}) collective-permute-start(f32[8,512]{1,0:T(8,128)S(1)} %copy-done.7), channel_id=1, source_target_pairs={{0,1},{1,2},{2,3},{3,4},{4,5},{5,6},{6,7},{7,0},{8,9},{9,10},{10,1... | collective-permute-start | bytes 49160 | tf_op jit(solution)/shard_map/ppermute | solution.py:22
  124.9 5.0 %collective-permute-start.1 = (f32[8,512]{1,0:T(8,128)S(1)}, f32[8,512]{1,0:T(8,128)S(1)}, u32[]{:S(2)}, u32[]{:S(2)}) collective-permute-start(f32[8,512]{1,0:T(8,128)S(1)} %collective-permute-done), channel_id=1, source_target_pairs={{0,1},{1,2},{2,3},{3,4},{4,5},{5,6},{6,7},{7,0},{8,9},{9,10},{10,1... | collective-permute-start | bytes 49160 | tf_op jit(solution)/shard_map/ppermute | solution.py:22
  129.9 5.0 %collective-permute-start.2 = (f32[8,512]{1,0:T(8,128)S(1)}, f32[8,512]{1,0:T(8,128)S(1)}, u32[]{:S(2)}, u32[]{:S(2)}) collective-permute-start(f32[8,512]{1,0:T(8,128)S(1)} %collective-permute-done.1), channel_id=1, source_target_pairs={{0,1},{1,2},{2,3},{3,4},{4,5},{5,6},{6,7},{7,0},{8,9},{9,10},{10,1... | collective-permute-start | bytes 49160 | tf_op jit(solution)/shard_map/ppermute | solution.py:22
  134.8 5.0 %collective-permute-start.3 = (f32[8,512]{1,0:T(8,128)S(1)}, f32[8,512]{1,0:T(8,128)S(1)}, u32[]{:S(2)}, u32[]{:S(2)}) collective-permute-start(f32[8,512]{1,0:T(8,128)S(1)} %collective-permute-done.2), channel_id=1, source_target_pairs={{0,1},{1,2},{2,3},{3,4},{4,5},{5,6},{6,7},{7,0},{8,9},{9,10},{10,1... | collective-permute-start | bytes 49160 | tf_op jit(solution)/shard_map/ppermute | solution.py:22
  139.8 5.0 %collective-permute-start.4 = (f32[8,512]{1,0:T(8,128)S(1)}, f32[8,512]{1,0:T(8,128)S(1)}, u32[]{:S(2)}, u32[]{:S(2)}) collective-permute-start(f32[8,512]{1,0:T(8,128)S(1)} %collective-permute-done.3), channel_id=1, source_target_pairs={{0,1},{1,2},{2,3},{3,4},{4,5},{5,6},{6,7},{7,0},{8,9},{9,10},{10,1... | collective-permute-start | bytes 49160 | tf_op jit(solution)/shard_map/ppermute | solution.py:22
  144.8 5.0 %collective-permute-start.5 = (f32[8,512]{1,0:T(8,128)S(1)}, f32[8,512]{1,0:T(8,128)S(1)}, u32[]{:S(2)}, u32[]{:S(2)}) collective-permute-start(f32[8,512]{1,0:T(8,128)S(1)} %collective-permute-done.4), channel_id=1, source_target_pairs={{0,1},{1,2},{2,3},{3,4},{4,5},{5,6},{6,7},{7,0},{8,9},{9,10},{10,1... | collective-permute-start | bytes 49160 | tf_op jit(solution)/shard_map/ppermute | solution.py:22
  149.7 5.0 %collective-permute-start.6 = (f32[8,512]{1,0:T(8,128)S(1)}, f32[8,512]{1,0:T(8,128)S(1)}, u32[]{:S(2)}, u32[]{:S(2)}) collective-permute-start(f32[8,512]{1,0:T(8,128)S(1)} %collective-permute-done.5), channel_id=1, source_target_pairs={{0,1},{1,2},{2,3},{3,4},{4,5},{5,6},{6,7},{7,0},{8,9},{9,10},{10,1... | collective-permute-start | bytes 49160 | tf_op jit(solution)/shard_map/ppermute | solution.py:22
  149.7 50.1 %collective-permute-start.8 = (bf16[8,512,512]{2,1,0:T(8,128)(2,1)}, bf16[8,512,512]{2,1,0:T(8,128)(2,1)}, u32[]{:S(2)}, u32[]{:S(2)}) collective-permute-start(bf16[8,512,512]{2,1,0:T(8,128)(2,1)} %collective-permute-done.7), channel_id=1, source_target_pairs={{0,1},{1,2},{2,3},{3,4},{4,5},{5,6},{6,7},{7,0},{8,9},{9,10},{10,1... | collective-permute-start | bytes 12582920 | tf_op jit(solution)/shard_map/ppermute | solution.py:11
  174.1 25.8 %copy-start = (bf16[512,8,512]{2,0,1:T(8,128)(2,1)S(1)}, bf16[512,8,512]{2,0,1:T(8,128)(2,1)}, u32[]{:S(2)}) copy-start(bf16[512,8,512]{2,0,1:T(8,128)(2,1)} %reshape.170) | copy-start | bytes 12582916
  199.8 50.0 %collective-permute-start.9 = (bf16[8,512,512]{2,1,0:T(8,128)(2,1)}, bf16[8,512,512]{2,1,0:T(8,128)(2,1)}, u32[]{:S(2)}, u32[]{:S(2)}) collective-permute-start(bf16[8,512,512]{2,1,0:T(8,128)(2,1)} %collective-permute-done.8), channel_id=1, source_target_pairs={{0,1},{1,2},{2,3},{3,4},{4,5},{5,6},{6,7},{7,0},{8,9},{9,10},{10,1... | collective-permute-start | bytes 12582920 | tf_op jit(solution)/shard_map/ppermute | solution.py:11
  200.1 1.3 copy-start.5
  212.6 7.4 %copy-start.1 = (bf16[512,8,512]{2,0,1:T(8,128)(2,1)S(1)}, bf16[512,8,512]{2,0,1:T(8,128)(2,1)}, u32[]{:S(2)}) copy-start(bf16[512,8,512]{2,0,1:T(8,128)(2,1)} %reshape.170) | copy-start | bytes 12582916
  233.7 23.4 %copy-start.2 = (bf16[512,8,512]{2,0,1:T(8,128)(2,1)S(1)}, bf16[512,8,512]{2,0,1:T(8,128)(2,1)}, u32[]{:S(2)}) copy-start(bf16[512,8,512]{2,0,1:T(8,128)(2,1)} %reshape.170) | copy-start | bytes 12582916
  249.8 50.0 %collective-permute-start.10 = (bf16[8,512,512]{2,1,0:T(8,128)(2,1)}, bf16[8,512,512]{2,1,0:T(8,128)(2,1)}, u32[]{:S(2)}, u32[]{:S(2)}) collective-permute-start(bf16[8,512,512]{2,1,0:T(8,128)(2,1)} %collective-permute-done.9), channel_id=1, source_target_pairs={{0,1},{1,2},{2,3},{3,4},{4,5},{5,6},{6,7},{7,0},{8,9},{9,10},{10,1... | collective-permute-start | bytes 12582920 | tf_op jit(solution)/shard_map/ppermute | solution.py:11
  270.8 7.4 %copy-start.3 = (bf16[512,8,512]{2,0,1:T(8,128)(2,1)S(1)}, bf16[512,8,512]{2,0,1:T(8,128)(2,1)}, u32[]{:S(2)}) copy-start(bf16[512,8,512]{2,0,1:T(8,128)(2,1)} %reshape.170) | copy-start | bytes 12582916
  292.0 15.2 %copy-start.4 = (bf16[512,8,512]{2,0,1:T(8,128)(2,1)S(1)}, bf16[512,8,512]{2,0,1:T(8,128)(2,1)}, u32[]{:S(2)}) copy-start(bf16[512,8,512]{2,0,1:T(8,128)(2,1)} %reshape.170) | copy-start | bytes 12582916
